TPU v7x, 32 devices: a whole 2x2x4 slice. The times are simulated.
32 devices in a mesh: dp: 8 (over z, core), tensor: 4 (over y, x).
Axes of the slice: x: 2, y: 2, z: 4, core: 2. Of those that a mesh axis runs over, the one named last changes fastest.
Arguments:
- tokens: bfloat16 [1024, 2048], P(('dp', 'tensor')), may hold values from -6 to 6
- gate_weight: bfloat16 [2048, 8192], P(None, 'tensor'), may hold values from -0.125 to 0.125
- up_act: bfloat16 [1024, 8192], P('dp', 'tensor'), may hold values from -6 to 6
- cotangent: bfloat16 [1024, 8192], P('dp', 'tensor'), may hold values from -6 to 6
- moment1: bfloat16 [2048, 8192], P('dp', 'tensor'), may hold values from -0.359375 to 0.359375
- moment2: bfloat16 [2048, 8192], P('dp', 'tensor'), may hold values from 0.0039978027 to 0.039794922
Outputs:
- in_grad: bfloat16 [1024, 2048], P(('dp', 'tensor'))
- up_grad: bfloat16 [1024, 8192], P('dp', 'tensor')
- new_moment1: bfloat16 [2048, 8192], P('dp', 'tensor')
- new_moment2: bfloat16 [2048, 8192], P('dp', 'tensor')
- update: float32 [2048, 8192], P('dp', 'tensor')
All inputs are finite; a program needn't handle non-finite values.
Results may differ from a plain program's by a relative error of at most 0.015.
Values may be sent and summed in bfloat16 or wider, within the bound.
No kernel may reach another device: no remote copies, remote signals or barrier semaphores. Data moves between devices by JAX's collectives and lax.ppermute only.
A program may use at most 64 MiB of HBM per device.

v0:
```python
import math

import jax
import jax.numpy as jnp
from jax import lax
from jax.sharding import PartitionSpec as P


def local(tokens, gate_weight, up_act, cotangent, moment1, moment2):
    gathered = lax.all_gather(tokens, "tensor", axis=0, tiled=True)
    gate_pre = jnp.dot(gathered, gate_weight, preferred_element_type=jnp.float32)
    sigmoid_gate = jax.nn.sigmoid(gate_pre)
    cot_float = cotangent.astype(jnp.float32)
    up_grad = (cot_float * gate_pre * sigmoid_gate).astype(jnp.bfloat16)
    gate_grad = (
        cot_float
        * up_act.astype(jnp.float32)
        * sigmoid_gate
        * (1.0 + gate_pre * (1.0 - sigmoid_gate))
    ).astype(jnp.bfloat16)
    in_grad = lax.psum_scatter(
        lax.dot_general(
            gate_grad, gate_weight, (((1,), (1,)), ((), ())), preferred_element_type=jnp.float32
        ).astype(jnp.bfloat16),
        "tensor",
        scatter_dimension=0,
        tiled=True,
    )
    partial_value = lax.dot_general(
        gathered, gate_grad, (((0,), (0,)), ((), ())), preferred_element_type=jnp.float32
    ).astype(jnp.bfloat16)
    grad_shard = lax.psum_scatter(
        partial_value.astype(jnp.float32), "dp", scatter_dimension=0, tiled=True
    )
    grad_scale = 1.0 / math.sqrt(lax.axis_size("dp") * gathered.shape[0])
    grad = grad_shard * grad_scale
    first = 0.9 * moment1.astype(jnp.float32) + 0.1 * grad
    second = 0.95 * moment2.astype(jnp.float32) + 0.05 * grad * grad
    update = first / (jnp.sqrt(second) + 1e-08)
    return (in_grad, up_grad, first.astype(jnp.bfloat16), second.astype(jnp.bfloat16), update)


def solution(mesh):
    placed = (
        P(("dp", "tensor"), None),
        P(None, "tensor"),
        P("dp", "tensor"),
        P("dp", "tensor"),
        P("dp", "tensor"),
        P("dp", "tensor"),
    )
    return jax.shard_map(
        local,
        mesh=mesh,
        in_specs=placed,
        out_specs=(
            P(("dp", "tensor"), None),
            P("dp", "tensor"),
            P("dp", "tensor"),
            P("dp", "tensor"),
            P("dp", "tensor"),
        ),
        check_vma=False,
    )
```

profile of v0, /device:TPU:0, one launch (start us, length us, event | category | flops | bytes accessed | tf_op | source)
XLA Modules:
  0.0 235.8 jit_solution(7843654203458309220)
XLA Ops:
  7.2 0.0 reduce-scatter.5.cloned.1.call-start
  7.2 11.9 %all_gather.3 = bf16[128,2048]{1,0:T(8,128)(2,1)S(1)} all-gather(bf16[32,2048]{1,0:T(8,128)(2,1)} %param.6), channel_id=1, replica_groups=mesh['dp'=8,'tensor'=4] {'tensor'}, dimensions={0}, use_global_device_ids=true | all-gather | bytes 655360 | tf_op jit(solution)/shard_map/all_gather | solution.py:10
  19.1 6.2 %fusion.5 = (bf16[128,2048]{1,0:T(8,128)(2,1)}, bf16[128,2048]{1,0:T(8,128)(2,1)S(1)}) fusion(bf16[128,2048]{1,0:T(8,128)(2,1)} %param.9, bf16[128,2048]{1,0:T(8,128)(2,1)} %param.8, bf16[128,2048]{1,0:T(8,128)(2,1)S(1)} %all_gather.3, bf16[2048,2048]{1,0:T(8,128)(2,1)} %param.7), kind=kOutput, calls=%fused_computation.12 | convolution fusion | flops 1077673984 | bytes 11010048 | tf_op jit(solution)/shard_map/dot_general | solution.py:11
  25.3 8.1 %convert_bitcast_fusion = f32[2048,2048]{0,1:T(8,128)} fusion(bf16[128,2048]{1,0:T(8,128)(2,1)S(1)} %get-tuple-element.14, bf16[128,2048]{1,0:T(8,128)(2,1)S(1)} %all_gather.3), kind=kOutput, calls=%fused_computation | convolution fusion | flops 1082130432 | bytes 17825792 | tf_op jit(solution)/shard_map/dot_general | solution.py:29
  33.4 0.0 reduce-scatter.5.cloned.1.call-update
  33.4 0.0 copy-start.1
  33.4 0.0 reduce-scatter.3.cloned.1.call-start
  33.5 7.1 %convolution_convert_fusion = bf16[128,2048]{1,0:T(8,128)(2,1)} fusion(bf16[128,2048]{1,0:T(8,128)(2,1)S(1)} %get-tuple-element.14, bf16[2048,2048]{1,0:T(8,128)(2,1)} %param.7), kind=kOutput, calls=%fused_computation.1 | convolution fusion | flops 1074003968 | bytes 9437184 | tf_op jit(solution)/shard_map/dot_general | solution.py:22
  40.6 0.0 reduce-scatter.3.cloned.1.call-update
  40.6 0.0 copy-done.1
  40.6 0.5 copy.11
  41.2 2.3 copy.12
  43.4 158.6 %reduce-scatter.5.cloned.1.call-done = f32[256,2048]{0,1:T(8,128)} async-done(((f32[2048,2048]{0,1:T(8,128)}), f32[256,2048]{0,1:T(8,128)}) %reduce-scatter.5.cloned.1.call-update) | async-done | bytes 2097168 | tf_op jit(solution)/shard_map/reduce_scatter | solution.py:32
  202.0 4.6 %add_divide_fusion = (f32[256,2048]{0,1:T(8,128)S(1)}, bf16[256,2048]{0,1:T(8,128)(2,1)}, bf16[256,2048]{0,1:T(8,128)(2,1)}) fusion(f32[256,2048]{0,1:T(8,128)} %reduce-scatter.5.cloned.1.call-done, bf16[256,2048]{0,1:T(8,128)(2,1)S(1)} %copy.11, bf16[256,2048]{0,1:T(8,128)(2,1)} %copy.12), kind=kLoop, calls=%fused_computation.2 | loop fusion | flops 7340032 | bytes 8388608 | tf_op jit(solution)/shard_map/div | solution.py:39
  206.6 0.0 copy-start
  206.6 2.4 copy.13
  208.9 0.0 copy-done
  208.9 1.4 copy.14
  210.4 1.8 copy.15
  212.2 16.8 %reduce-scatter.3.cloned.1.call-done = bf16[32,2048]{1,0:T(8,128)(2,1)} async-done(((bf16[128,2048]{1,0:T(8,128)(2,1)}), bf16[32,2048]{1,0:T(8,128)(2,1)}) %reduce-scatter.3.cloned.1.call-update) | async-done | bytes 131088 | tf_op jit(solution)/shard_map/reduce_scatter | solution.py:21
Async XLA Ops:
  7.2 194.8 %reduce-scatter.5.cloned.1.call-start = ((), (), s32[]{:S(2)}) async-start(), calls=%async_computation.3 | async-start | bytes 18874368 | tf_op jit(solution)/shard_map/reduce_scatter | solution.py:32
  33.4 7.2 %copy-start.1 = (bf16[256,2048]{1,0:T(8,128)(2,1)S(1)}, bf16[256,2048]{1,0:T(8,128)(2,1)}, u32[]{:S(2)}) copy-start(bf16[256,2048]{1,0:T(8,128)(2,1)} %param.10) | copy-start | bytes 3145732
  33.4 195.5 %reduce-scatter.3.cloned.1.call-start = ((), (), s32[]{:S(2)}) async-start(), calls=%async_computation.2 | async-start | bytes 655360 | tf_op jit(solution)/shard_map/reduce_scatter | solution.py:21
  206.6 2.4 copy-start
Sparse Core Ops, SparseCore 0:
  33.5 168.4 reduce-scatter.4
  205.4 23.5 reduce-scatter.2
where the time goes:
time: 236 us
  waiting for transfers between devices  175 us (74%)
  matrix products  21.4 us (9%)
  between operations  14.1 us (6%)
  blocking collectives  11.9 us (5%)
  local copies, waits for them, and re-layouts  8.37 us (4%)
  other arithmetic  4.59 us (2%)
    reduce_scatter x1, waiting for transfers between devices, local(): lax.psum_scatter(partial_value.astype(jnp.float32), 'dp', scatter_dimensi...  159 us
    reduce_scatter x1, waiting for transfers between devices, local(): lax.psum_scatter(lax.dot_general(gate_grad, gate_weight, (((1,), (1,)), (...  16.8 us
    all_gather x1, blocking collectives, local(): gathered = lax.all_gather(tokens, 'tensor', axis=0, tiled=True)  11.9 us
    unnamed x9, local copies, waits for them, and re-layouts  8.37 us
    dot_general x1, matrix products, local(): lax.dot_general(gathered, gate_grad, (((0,), (0,)), ((), ())), preferred_...  8.09 us
    dot_general x1, matrix products, local(): lax.dot_general(gate_grad, gate_weight, (((1,), (1,)), ((), ())), preferr...  7.13 us
    dot_general x1, matrix products, local(): jnp.dot(gathered, gate_weight, preferred_element_type=jnp.float32)  6.2 us
  transfers between devices with their start and end apart: 2, of which 2 were waited for; matrix products, arithmetic and copies ran while one was open for 9% of the time, Pallas kernels for 0%

commit v1 on v0

v1 whole, which is shorter than its diff:
```python
import math

import jax
import jax.numpy as jnp
from jax import lax
from jax.sharding import PartitionSpec as P

CHUNKS = 4


def activation(tokens_all, gate_weight, up_act, cotangent):
    gate_pre = jnp.dot(tokens_all, gate_weight, preferred_element_type=jnp.float32)
    sig = jax.nn.sigmoid(gate_pre)
    cot = cotangent.astype(jnp.float32)
    up_grad = (cot * gate_pre * sig).astype(jnp.bfloat16)
    gate_grad = (cot * up_act.astype(jnp.float32) * sig * (1.0 + gate_pre * (1.0 - sig))).astype(
        jnp.bfloat16
    )
    return up_grad, gate_grad


def adam(grad, moment1, moment2):
    first = 0.9 * moment1.astype(jnp.float32) + 0.1 * grad
    second = 0.95 * moment2.astype(jnp.float32) + 0.05 * grad * grad
    update = first / (jnp.sqrt(second) + 1e-08)
    return first.astype(jnp.bfloat16), second.astype(jnp.bfloat16), update


def dot_nt(a, b):
    return lax.dot_general(a, b, (((1,), (1,)), ((), ())), preferred_element_type=jnp.float32)


def dot_tn(a, b):
    return lax.dot_general(a, b, (((0,), (0,)), ((), ())), preferred_element_type=jnp.float32)


def reduced(tokens, gate_weight, up_act, cotangent, moment1, moment2):
    gathered = lax.all_gather(tokens, "tensor", axis=0, tiled=True)
    up_grad, gate_grad = activation(gathered, gate_weight, up_act, cotangent)
    in_grad = lax.psum_scatter(
        dot_nt(gate_grad, gate_weight).astype(jnp.bfloat16), "tensor", scatter_dimension=0, tiled=True
    )
    partial_value = dot_tn(gathered, gate_grad).astype(jnp.bfloat16)
    grad_shard = lax.psum_scatter(
        partial_value.astype(jnp.float32), "dp", scatter_dimension=0, tiled=True
    )
    grad = grad_shard * (1.0 / math.sqrt(lax.axis_size("dp") * gathered.shape[0]))
    return (in_grad, up_grad, *adam(grad, moment1, moment2))


def swapped(value, axis, k):
    return lax.ppermute(value, axis, [(i, i ^ k) for i in range(lax.axis_size(axis))])


def ordered(slots, me):
    out = []
    for j in range(len(slots)):
        cand = [slots[j ^ w] for w in range(len(slots))]
        bit = 1
        while len(cand) > 1:
            odd = (me & bit) != 0
            cand = [jnp.where(odd, cand[i + 1], cand[i]) for i in range(0, len(cand), 2)]
            bit *= 2
        out.append(cand[0])
    return out


def gathered_over(value, axis):
    slots = [value] + [swapped(value, axis, k) for k in range(1, lax.axis_size(axis))]
    return ordered(slots, lax.axis_index(axis))


def exchanged(tokens, gate_weight, up_act, cotangent, moment1, moment2):
    n, ways = lax.axis_size("dp"), lax.axis_size("tensor")
    chips = n // 2
    at, way = lax.axis_index("dp"), lax.axis_index("tensor")
    chip, core = at // 2, at % 2
    few, width = tokens.shape
    owned = moment1.shape[0]
    pair = 2 * owned
    cols = gate_weight.shape[1]

    gathered = jnp.concatenate(gathered_over(tokens, "tensor"), axis=0)

    def shift(value, s):
        return lax.ppermute(value, "dp", [(i, (i + 2 * s) % n) for i in range(n)])

    far = []
    for s in range(1, chips):
        to = (chip + s) % chips
        far.append(shift(lax.dynamic_slice_in_dim(tokens, to * pair, pair, 1), s))
    far = gathered_over(jnp.concatenate(far, axis=0), "tensor")

    up_grad, gate_grad = activation(gathered, gate_weight, up_act, cotangent)

    step = cols // CHUNKS
    parts = [[gate_grad[:, j * step : (j + 1) * step]] for j in range(CHUNKS)]
    for s in range(1, chips):
        for part in parts:
            part.append(shift(part[-1], 1))

    term = dot_nt(gate_grad, gate_weight).astype(jnp.bfloat16)
    block = lambda w: lax.dynamic_slice_in_dim(term, w * few, few, 0)
    total = block(way).astype(jnp.float32)
    for k in range(1, ways):
        total = total + swapped(block(way ^ k), "tensor", k).astype(jnp.float32)
    in_grad = total.astype(jnp.bfloat16)

    def rows_of(which):
        mine = lax.dynamic_slice_in_dim(gathered, (2 * chip + which) * owned, owned, 1)
        rest = [lax.dynamic_slice_in_dim(f, which * owned, owned, 1) for f in far]
        out = [mine]
        for s in range(1, chips):
            out.append(jnp.concatenate([r[(s - 1) * few : s * few] for r in rest], axis=0))
        return out

    own_rows, other_rows = rows_of(core), rows_of(1 - core)

    def product(rows, part):
        head = dot_tn(jnp.concatenate(rows[:-1], axis=0), jnp.concatenate(part[:-1], axis=0))
        return head + dot_tn(rows[-1], part[-1])

    scale = 1.0 / math.sqrt(n * gathered.shape[0])
    results = []
    for j, part in enumerate(parts):
        other = swapped(product(other_rows, part).astype(jnp.bfloat16), "dp", 1)
        grad = (product(own_rows, part) + other.astype(jnp.float32)) * scale
        sel = slice(j * step, (j + 1) * step)
        results.append(adam(grad, moment1[:, sel], moment2[:, sel]))
    new = [jnp.concatenate(list(r), axis=1) for r in zip(*results)]
    return (in_grad, up_grad, *new)


def local(tokens, gate_weight, up_act, cotangent, moment1, moment2):
    n, ways = lax.axis_size("dp"), lax.axis_size("tensor")
    total_tokens = n * up_act.shape[0]
    lighter = total_tokens * 2 <= gate_weight.shape[0] * 4
    if lighter and n % 2 == 0 and ways & (ways - 1) == 0:
        return exchanged(tokens, gate_weight, up_act, cotangent, moment1, moment2)
    return reduced(tokens, gate_weight, up_act, cotangent, moment1, moment2)


def solution(mesh):
    placed = (
        P(("dp", "tensor"), None),
        P(None, "tensor"),
        P("dp", "tensor"),
        P("dp", "tensor"),
        P("dp", "tensor"),
        P("dp", "tensor"),
    )
    return jax.shard_map(
        local,
        mesh=mesh,
        in_specs=placed,
        out_specs=(
            P(("dp", "tensor"), None),
            P("dp", "tensor"),
            P("dp", "tensor"),
            P("dp", "tensor"),
            P("dp", "tensor"),
        ),
        check_vma=False,
    )
```

time: 236 us -> 75.6 us (0.32)
  waiting for transfers between devices: 175 us -> 23.4 us
  starting transfers between devices: 0.08 us -> 28.9 us
  between operations: 14.1 us -> 1.07 us
  blocking collectives: 11.9 us -> 0 us
  local copies, waits for them, and re-layouts: 8.37 us -> 1.11 us
  matrix products: 21.4 us -> 16.1 us
    reduce_scatter x2 -> x0, waiting for transfers between devices: 175 us -> none  [the longest x1 159 us: local(): lax.psum_scatter(partial_value.astype(jnp.float32), 'dp', scatter_dimensi...]
    ppermute x0 -> x28, starting transfers between devices: none -> 28.9 us  [the longest x15 16.3 us: shift(): return lax.ppermute(value, 'dp', [(i, (i + 2 * s) % n) for i in range(n)])]
    ppermute x0 -> x28, waiting for transfers between devices: none -> 23.4 us  [the longest x15 22.4 us: shift(): return lax.ppermute(value, 'dp', [(i, (i + 2 * s) % n) for i in range(n)])]
    all_gather x1 -> x0, blocking collectives: 11.9 us -> none  [local(): gathered = lax.all_gather(tokens, 'tensor', axis=0, tiled=True)]
    unnamed x9 -> x17, local copies, waits for them, and re-layouts: 8.37 us -> 0.11 us
    dot_general x3 -> x18, matrix products: 21.4 us -> 16.1 us  [the longest x16 7.08 us: dot_tn(): lax.dot_general(a, b, (((0,), (0,)), ((), ())), preferred_element_type=jn...]
    div x1 -> x0, other arithmetic: 4.59 us -> none  [local(): update = first / (jnp.sqrt(second) + 1e-08)]
    concatenate x0 -> x3, other arithmetic: none -> 3.16 us  [the longest x2 3.12 us: exchanged(): new = [jnp.concatenate(list(r), axis=1) for r in zip(*results)]]
  transfers between devices with their start and end apart: 2 -> 28, of which waited for: 2 -> 11; matrix products, arithmetic and copies ran while one was open for 9% -> 20% of each run, Pallas kernels for 0% -> 0%
where the time goes in v1:
time: 75.6 us; the launch traced here: 75.5 us
  starting transfers between devices  28.9 us (38%)
  waiting for transfers between devices  23.4 us (31%)
  matrix products  16.1 us (21%)
  other arithmetic  4.87 us (6%)
  local copies, waits for them, and re-layouts  1.11 us (1%)
  between operations  1.07 us (1%)
    ppermute x15, waiting for transfers between devices, shift(): return lax.ppermute(value, 'dp', [(i, (i + 2 * s) % n) for i in range(n)])  22.4 us
    ppermute x15, starting transfers between devices, shift(): return lax.ppermute(value, 'dp', [(i, (i + 2 * s) % n) for i in range(n)])  16.3 us
    ppermute x13, starting transfers between devices, swapped(): lax.ppermute(value, axis, [(i, i ^ k) for i in range(lax.axis_size(axis))])  12.6 us
    dot_general x16, matrix products, dot_tn(): lax.dot_general(a, b, (((0,), (0,)), ((), ())), preferred_element_type=jn...  7.08 us
    dot_general x1, matrix products, activation(): jnp.dot(tokens_all, gate_weight, preferred_element_type=jnp.float32)  6.18 us
    concatenate x2, other arithmetic, exchanged(): new = [jnp.concatenate(list(r), axis=1) for r in zip(*results)]  3.12 us
    dot_general x1, matrix products, dot_nt(): lax.dot_general(a, b, (((1,), (1,)), ((), ())), preferred_element_type=jn...  2.88 us
  transfers between devices with their start and end apart: 28, of which 11 were waited for; matrix products, arithmetic and copies ran while one was open for 20% of the time, Pallas kernels for 0%

profile of v1, /device:TPU:0, one launch (start us, length us, event | category | flops | bytes accessed | tf_op | source)
XLA Modules:
  0.0 75.5 jit_solution(14006637955153038802)
XLA Ops:
  1.6 3.1 %collective-permute-start.6 = (bf16[32,512]{1,0:T(8,128)(2,1)S(1)}, bf16[32,512]{1,0:T(8,128)(2,1)S(1)}, u32[]{:S(2)}, u32[]{:S(2)}) collective-permute-start(bf16[32,512]{1,0:T(8,128)(2,1)S(1)} %get-tuple-element.36), channel_id=1, source_target_pairs={{0,8},{4,12},{8,16},{12,20},{16,24},{20,28},{24,0},{28,4},{1,9},{5... | collective-permute-start | bytes 98312 | tf_op jit(solution)/shard_map/ppermute | solution.py:86
  4.7 1.5 %collective-permute-start.2 = (bf16[32,2048]{1,0:T(8,128)(2,1)}, bf16[32,2048]{1,0:T(8,128)(2,1)S(1)}, u32[]{:S(2)}, u32[]{:S(2)}) collective-permute-start(bf16[32,2048]{1,0:T(8,128)(2,1)} %param.6), channel_id=1, source_target_pairs={{0,1},{1,0},{2,3},{3,2},{4,5},{5,4},{6,7},{7,6},{8,9},{9,8},{10,11... | collective-permute-start | bytes 393224 | tf_op jit(solution)/shard_map/ppermute | solution.py:52
  6.2 1.5 %collective-permute-start.1 = (bf16[32,2048]{1,0:T(8,128)(2,1)}, bf16[32,2048]{1,0:T(8,128)(2,1)S(1)}, u32[]{:S(2)}, u32[]{:S(2)}) collective-permute-start(bf16[32,2048]{1,0:T(8,128)(2,1)} %param.6), channel_id=1, source_target_pairs={{0,2},{1,3},{2,0},{3,1},{4,6},{5,7},{6,4},{7,5},{8,10},{9,11},{10,... | collective-permute-start | bytes 393224 | tf_op jit(solution)/shard_map/ppermute | solution.py:52
  8.2 2.1 %collective-permute-start.8 = (bf16[32,512]{1,0:T(8,128)(2,1)S(1)}, bf16[32,512]{1,0:T(8,128)(2,1)S(1)}, u32[]{:S(2)}, u32[]{:S(2)}) collective-permute-start(bf16[32,512]{1,0:T(8,128)(2,1)S(1)} %get-tuple-element.35), channel_id=1, source_target_pairs={{0,24},{4,28},{8,0},{12,4},{16,8},{20,12},{24,16},{28,20},{1,25},{... | collective-permute-start | bytes 98312 | tf_op jit(solution)/shard_map/ppermute | solution.py:86
  11.2 3.9 %collective-permute-done.7 = bf16[32,512]{1,0:T(8,128)(2,1)S(1)} collective-permute-done((bf16[32,512]{1,0:T(8,128)(2,1)S(1)}, bf16[32,512]{1,0:T(8,128)(2,1)S(1)}, u32[]{:S(2)}, u32[]{:S(2)}) %collective-permute-start.7) | collective-permute-done | bytes 32800 | tf_op jit(solution)/shard_map/ppermute | solution.py:86
  15.1 1.7 %collective-permute-start.11 = (bf16[96,512]{1,0:T(8,128)(2,1)S(1)}, bf16[96,512]{1,0:T(8,128)(2,1)S(1)}, u32[]{:S(2)}, u32[]{:S(2)}) collective-permute-start(bf16[96,512]{1,0:T(8,128)(2,1)S(1)} %constant_dynamic-update-slice_fusion), channel_id=1, source_target_pairs={{0,1},{1,0},{2,3},{3,2},{4,5},{5,4},{6,7},{7,6},{8,9},{9,8},{10,11... | collective-permute-start | bytes 294920 | tf_op jit(solution)/shard_map/ppermute | solution.py:52
  16.8 1.5 %collective-permute-start.10 = (bf16[96,512]{1,0:T(8,128)(2,1)S(1)}, bf16[96,512]{1,0:T(8,128)(2,1)S(1)}, u32[]{:S(2)}, u32[]{:S(2)}) collective-permute-start(bf16[96,512]{1,0:T(8,128)(2,1)S(1)} %constant_dynamic-update-slice_fusion), channel_id=1, source_target_pairs={{0,2},{1,3},{2,0},{3,1},{4,6},{5,7},{6,4},{7,5},{8,10},{9,11},{10,... | collective-permute-start | bytes 294920 | tf_op jit(solution)/shard_map/ppermute | solution.py:52
  19.7 6.2 %fusion.12 = (bf16[128,2048]{1,0:T(8,128)(2,1)}, bf16[128,2048]{1,0:T(8,128)(2,1)S(1)}) fusion(bf16[128,2048]{1,0:T(8,128)(2,1)S(1)} %copy-done.1, bf16[128,2048]{1,0:T(8,128)(2,1)S(1)} %copy-done.2, bf16[2048,2048]{1,0:T(8,128)(2,1)} %param.7, bf16[32,2048]{1,0:T(8,128)(2,1)S(1)} %get-tuple-element.30, bf16[32,2048]{1,0:T(8,128)(2,1)S(1)} %get-tuple-element.29, ...), kind=kOutput, calls=%fused_computation.24 | convolution fusion | flops 1079771136 | bytes 11010048 | tf_op jit(solution)/shard_map/dot_general | solution.py:12
  25.9 2.9 %convolution_convert_fusion = bf16[128,2048]{1,0:T(8,128)(2,1)S(1)} fusion(bf16[128,2048]{1,0:T(8,128)(2,1)S(1)} %get-tuple-element.17, bf16[2048,2048]{1,0:T(8,128)(2,1)S(1)} %bitcast.20), kind=kOutput, calls=%fused_computation | convolution fusion | flops 1074003968 | bytes 9437184 | tf_op jit(solution)/shard_map/dot_general | solution.py:30
  28.9 1.5 %collective-permute-start.24 = (bf16[128,512]{1,0:T(8,128)(2,1)S(1)}, bf16[128,512]{1,0:T(8,128)(2,1)S(1)}, u32[]{:S(2)}, u32[]{:S(2)}) collective-permute-start(bf16[128,512]{1,0:T(8,128)(2,1)S(1)} %get-tuple-element.19), channel_id=1, source_target_pairs={{0,8},{4,12},{8,16},{12,20},{16,24},{20,28},{24,0},{28,4},{1,9},{5... | collective-permute-start | bytes 393224 | tf_op jit(solution)/shard_map/ppermute | solution.py:86
  30.5 1.8 %collective-permute-start.20 = (bf16[128,512]{1,0:T(8,128)(2,1)S(1)}, bf16[128,512]{1,0:T(8,128)(2,1)S(1)}, u32[]{:S(2)}, u32[]{:S(2)}) collective-permute-start(bf16[128,512]{1,0:T(8,128)(2,1)S(1)} %get-tuple-element.20), channel_id=1, source_target_pairs={{0,8},{4,12},{8,16},{12,20},{16,24},{20,28},{24,0},{28,4},{1,9},{5... | collective-permute-start | bytes 393224 | tf_op jit(solution)/shard_map/ppermute | solution.py:86
  32.4 1.6 %collective-permute-start.16 = (bf16[128,512]{1,0:T(8,128)(2,1)S(1)}, bf16[128,512]{1,0:T(8,128)(2,1)S(1)}, u32[]{:S(2)}, u32[]{:S(2)}) collective-permute-start(bf16[128,512]{1,0:T(8,128)(2,1)S(1)} %get-tuple-element.21), channel_id=1, source_target_pairs={{0,8},{4,12},{8,16},{12,20},{16,24},{20,28},{24,0},{28,4},{1,9},{5... | collective-permute-start | bytes 393224 | tf_op jit(solution)/shard_map/ppermute | solution.py:86
  34.0 1.6 %collective-permute-start.3 = (bf16[32,2048]{1,0:T(8,128)(2,1)S(1)}, bf16[32,2048]{1,0:T(8,128)(2,1)S(1)}, u32[]{:S(2)}, u32[]{:S(2)}) collective-permute-start(bf16[32,2048]{1,0:T(8,128)(2,1)S(1)} %get-tuple-element.24), channel_id=1, source_target_pairs={{0,1},{1,0},{2,3},{3,2},{4,5},{5,4},{6,7},{7,6},{8,9},{9,8},{10,11... | collective-permute-start | bytes 393224 | tf_op jit(solution)/shard_map/ppermute | solution.py:52
  37.1 2.5 %collective-permute-start.5 = (bf16[32,2048]{1,0:T(8,128)(2,1)S(1)}, bf16[32,2048]{1,0:T(8,128)(2,1)S(1)}, u32[]{:S(2)}, u32[]{:S(2)}) collective-permute-start(bf16[32,2048]{1,0:T(8,128)(2,1)S(1)} %get-tuple-element.25), channel_id=1, source_target_pairs={{0,3},{1,2},{2,1},{3,0},{4,7},{5,6},{6,5},{7,4},{8,11},{9,10},{10,... | collective-permute-start | bytes 393224 | tf_op jit(solution)/shard_map/ppermute | solution.py:52
  41.0 2.8 %collective-permute-done.16 = bf16[128,512]{1,0:T(8,128)(2,1)S(1)} collective-permute-done((bf16[128,512]{1,0:T(8,128)(2,1)S(1)}, bf16[128,512]{1,0:T(8,128)(2,1)S(1)}, u32[]{:S(2)}, u32[]{:S(2)}) %collective-permute-start.16) | collective-permute-done | bytes 131104 | tf_op jit(solution)/shard_map/ppermute | solution.py:86
  45.2 1.4 %collective-permute-start.17 = (bf16[128,512]{1,0:T(8,128)(2,1)S(1)}, bf16[128,512]{1,0:T(8,128)(2,1)S(1)}, u32[]{:S(2)}, u32[]{:S(2)}) collective-permute-start(bf16[128,512]{1,0:T(8,128)(2,1)S(1)} %collective-permute-done.16), channel_id=1, source_target_pairs={{0,8},{4,12},{8,16},{12,20},{16,24},{20,28},{24,0},{28,4},{1,9},{5... | collective-permute-start | bytes 393224 | tf_op jit(solution)/shard_map/ppermute | solution.py:86
  47.4 6.5 %collective-permute-done.21 = bf16[128,512]{1,0:T(8,128)(2,1)S(1)} collective-permute-done((bf16[128,512]{1,0:T(8,128)(2,1)S(1)}, bf16[128,512]{1,0:T(8,128)(2,1)S(1)}, u32[]{:S(2)}, u32[]{:S(2)}) %collective-permute-start.21) | collective-permute-done | bytes 131104 | tf_op jit(solution)/shard_map/ppermute | solution.py:86
  53.9 2.8 %collective-permute-done.17 = bf16[128,512]{1,0:T(8,128)(2,1)S(1)} collective-permute-done((bf16[128,512]{1,0:T(8,128)(2,1)S(1)}, bf16[128,512]{1,0:T(8,128)(2,1)S(1)}, u32[]{:S(2)}, u32[]{:S(2)}) %collective-permute-start.17) | collective-permute-done | bytes 131104 | tf_op jit(solution)/shard_map/ppermute | solution.py:86
  59.0 1.9 %collective-permute-start.14 = (bf16[128,512]{1,0:T(8,128)(2,1)S(1)}, bf16[128,512]{1,0:T(8,128)(2,1)S(1)}, u32[]{:S(2)}, u32[]{:S(2)}) collective-permute-start(bf16[128,512]{1,0:T(8,128)(2,1)S(1)} %collective-permute-done.13), channel_id=1, source_target_pairs={{0,8},{4,12},{8,16},{12,20},{16,24},{20,28},{24,0},{28,4},{1,9},{5... | collective-permute-start | bytes 393224 | tf_op jit(solution)/shard_map/ppermute | solution.py:86
  61.6 1.9 %collective-permute-done.18 = bf16[128,512]{1,0:T(8,128)(2,1)S(1)} collective-permute-done((bf16[128,512]{1,0:T(8,128)(2,1)S(1)}, bf16[128,512]{1,0:T(8,128)(2,1)S(1)}, u32[]{:S(2)}, u32[]{:S(2)}) %collective-permute-start.18) | collective-permute-done | bytes 131104 | tf_op jit(solution)/shard_map/ppermute | solution.py:86
  63.8 2.5 %collective-permute-done.14 = bf16[128,512]{1,0:T(8,128)(2,1)S(1)} collective-permute-done((bf16[128,512]{1,0:T(8,128)(2,1)S(1)}, bf16[128,512]{1,0:T(8,128)(2,1)S(1)}, u32[]{:S(2)}, u32[]{:S(2)}) %collective-permute-start.14) | collective-permute-done | bytes 131104 | tf_op jit(solution)/shard_map/ppermute | solution.py:86
  69.5 2.8 %add_divide_fusion.4 = (f32[256,512]{1,0:T(8,128)S(1)}, f32[256,512]{1,0:T(8,128)S(1)}, f32[256,512]{1,0:T(8,128)S(1)}, f32[256,512]{1,0:T(8,128)S(1)}, bf16[256...) fusion(f32[256,512]{1,0:T(8,128)S(1)} %get-tuple-element.63, ...), kind=kOutput, calls=%fused_computation.32 | convolution fusion | flops 41418752 | bytes 8585216 | tf_op jit(solution)/shard_map/dot_general | solution.py:34
  72.3 1.5 %pad_maximum_fusion = f32[256,2048]{1,0:T(8,128)} fusion(f32[256,512]{1,0:T(8,128)S(1)} %get-tuple-element.8, f32[256,512]{1,0:T(8,128)S(1)} %get-tuple-element.7, f32[256,512]{1,0:T(8,128)S(1)} %get-tuple-element.6, f32[256,512]{1,0:T(8,128)S(1)} %get-tuple-element.5), kind=kLoop, calls=%fused_computation.1 | loop fusion | flops 1572864 | bytes 4194304 | tf_op jit(solution)/shard_map/concatenate | solution.py:130
  73.8 1.6 %pad_maximum_fusion.1 = (bf16[256,2048]{1,0:T(8,128)(2,1)}, bf16[256,2048]{1,0:T(8,128)(2,1)}) fusion(bf16[256,512]{1,0:T(8,128)(2,1)S(1)} %get-tuple-element.10, bf16[256,512]{1,0:T(8,128)(2,1)S(1)} %get-tuple-element.11, bf16[256,512]{1,0:T(8,128)(2,1)S(1)} %get-tuple-element.9, bf16[256,512]{1,0:T(8,128)(2,1)S(1)} %get-tuple-element.62, ...), kind=kLoop, calls=%fused_computation.25 | loop fusion | flops 8388608 | bytes 4194304 | tf_op jit(solution)/shard_map/concatenate | solution.py:130
  (82 shorter events, 15.2 us)
Async XLA Ops:
  1.6 8.7 %collective-permute-start.6 = (bf16[32,512]{1,0:T(8,128)(2,1)S(1)}, bf16[32,512]{1,0:T(8,128)(2,1)S(1)}, u32[]{:S(2)}, u32[]{:S(2)}) collective-permute-start(bf16[32,512]{1,0:T(8,128)(2,1)S(1)} %get-tuple-element.36), channel_id=1, source_target_pairs={{0,8},{4,12},{8,16},{12,20},{16,24},{20,28},{24,0},{28,4},{1,9},{5... | collective-permute-start | bytes 98312 | tf_op jit(solution)/shard_map/ppermute | solution.py:86
  4.7 13.6 %collective-permute-start.2 = (bf16[32,2048]{1,0:T(8,128)(2,1)}, bf16[32,2048]{1,0:T(8,128)(2,1)S(1)}, u32[]{:S(2)}, u32[]{:S(2)}) collective-permute-start(bf16[32,2048]{1,0:T(8,128)(2,1)} %param.6), channel_id=1, source_target_pairs={{0,1},{1,0},{2,3},{3,2},{4,5},{5,4},{6,7},{7,6},{8,9},{9,8},{10,11... | collective-permute-start | bytes 393224 | tf_op jit(solution)/shard_map/ppermute | solution.py:52
  6.2 12.5 %collective-permute-start.1 = (bf16[32,2048]{1,0:T(8,128)(2,1)}, bf16[32,2048]{1,0:T(8,128)(2,1)S(1)}, u32[]{:S(2)}, u32[]{:S(2)}) collective-permute-start(bf16[32,2048]{1,0:T(8,128)(2,1)} %param.6), channel_id=1, source_target_pairs={{0,2},{1,3},{2,0},{3,1},{4,6},{5,7},{6,4},{7,5},{8,10},{9,11},{10,... | collective-permute-start | bytes 393224 | tf_op jit(solution)/shard_map/ppermute | solution.py:52
  7.7 11.0 %collective-permute-start = (bf16[32,2048]{1,0:T(8,128)(2,1)}, bf16[32,2048]{1,0:T(8,128)(2,1)S(1)}, u32[]{:S(2)}, u32[]{:S(2)}) collective-permute-start(bf16[32,2048]{1,0:T(8,128)(2,1)} %param.6), channel_id=1, source_target_pairs={{0,3},{1,2},{2,1},{3,0},{4,7},{5,6},{6,5},{7,4},{8,11},{9,10},{10,... | collective-permute-start | bytes 393224 | tf_op jit(solution)/shard_map/ppermute | solution.py:52
  8.2 6.9 %collective-permute-start.8 = (bf16[32,512]{1,0:T(8,128)(2,1)S(1)}, bf16[32,512]{1,0:T(8,128)(2,1)S(1)}, u32[]{:S(2)}, u32[]{:S(2)}) collective-permute-start(bf16[32,512]{1,0:T(8,128)(2,1)S(1)} %get-tuple-element.35), channel_id=1, source_target_pairs={{0,24},{4,28},{8,0},{12,4},{16,8},{20,12},{24,16},{28,20},{1,25},{... | collective-permute-start | bytes 98312 | tf_op jit(solution)/shard_map/ppermute | solution.py:86
  15.1 15.4 %collective-permute-start.11 = (bf16[96,512]{1,0:T(8,128)(2,1)S(1)}, bf16[96,512]{1,0:T(8,128)(2,1)S(1)}, u32[]{:S(2)}, u32[]{:S(2)}) collective-permute-start(bf16[96,512]{1,0:T(8,128)(2,1)S(1)} %constant_dynamic-update-slice_fusion), channel_id=1, source_target_pairs={{0,1},{1,0},{2,3},{3,2},{4,5},{5,4},{6,7},{7,6},{8,9},{9,8},{10,11... | collective-permute-start | bytes 294920 | tf_op jit(solution)/shard_map/ppermute | solution.py:52
  16.8 15.5 %collective-permute-start.10 = (bf16[96,512]{1,0:T(8,128)(2,1)S(1)}, bf16[96,512]{1,0:T(8,128)(2,1)S(1)}, u32[]{:S(2)}, u32[]{:S(2)}) collective-permute-start(bf16[96,512]{1,0:T(8,128)(2,1)S(1)} %constant_dynamic-update-slice_fusion), channel_id=1, source_target_pairs={{0,2},{1,3},{2,0},{3,1},{4,6},{5,7},{6,4},{7,5},{8,10},{9,11},{10,... | collective-permute-start | bytes 294920 | tf_op jit(solution)/shard_map/ppermute | solution.py:52
  18.3 15.7 %collective-permute-start.9 = (bf16[96,512]{1,0:T(8,128)(2,1)S(1)}, bf16[96,512]{1,0:T(8,128)(2,1)S(1)}, u32[]{:S(2)}, u32[]{:S(2)}) collective-permute-start(bf16[96,512]{1,0:T(8,128)(2,1)S(1)} %constant_dynamic-update-slice_fusion), channel_id=1, source_target_pairs={{0,3},{1,2},{2,1},{3,0},{4,7},{5,6},{6,5},{7,4},{8,11},{9,10},{10,... | collective-permute-start | bytes 294920 | tf_op jit(solution)/shard_map/ppermute | solution.py:52
  28.9 8.2 %collective-permute-start.12 = (bf16[128,512]{1,0:T(8,128)(2,1)S(1)}, bf16[128,512]{1,0:T(8,128)(2,1)S(1)}, u32[]{:S(2)}, u32[]{:S(2)}) collective-permute-start(bf16[128,512]{1,0:T(8,128)(2,1)S(1)} %get-tuple-element.18), channel_id=1, source_target_pairs={{0,8},{4,12},{8,16},{12,20},{16,24},{20,28},{24,0},{28,4},{1,9},{5... | collective-permute-start | bytes 393224 | tf_op jit(solution)/shard_map/ppermute | solution.py:86
  28.9 10.7 %collective-permute-start.24 = (bf16[128,512]{1,0:T(8,128)(2,1)S(1)}, bf16[128,512]{1,0:T(8,128)(2,1)S(1)}, u32[]{:S(2)}, u32[]{:S(2)}) collective-permute-start(bf16[128,512]{1,0:T(8,128)(2,1)S(1)} %get-tuple-element.19), channel_id=1, source_target_pairs={{0,8},{4,12},{8,16},{12,20},{16,24},{20,28},{24,0},{28,4},{1,9},{5... | collective-permute-start | bytes 393224 | tf_op jit(solution)/shard_map/ppermute | solution.py:86
  30.5 10.5 %collective-permute-start.20 = (bf16[128,512]{1,0:T(8,128)(2,1)S(1)}, bf16[128,512]{1,0:T(8,128)(2,1)S(1)}, u32[]{:S(2)}, u32[]{:S(2)}) collective-permute-start(bf16[128,512]{1,0:T(8,128)(2,1)S(1)} %get-tuple-element.20), channel_id=1, source_target_pairs={{0,8},{4,12},{8,16},{12,20},{16,24},{20,28},{24,0},{28,4},{1,9},{5... | collective-permute-start | bytes 393224 | tf_op jit(solution)/shard_map/ppermute | solution.py:86
  32.4 11.4 %collective-permute-start.16 = (bf16[128,512]{1,0:T(8,128)(2,1)S(1)}, bf16[128,512]{1,0:T(8,128)(2,1)S(1)}, u32[]{:S(2)}, u32[]{:S(2)}) collective-permute-start(bf16[128,512]{1,0:T(8,128)(2,1)S(1)} %get-tuple-element.21), channel_id=1, source_target_pairs={{0,8},{4,12},{8,16},{12,20},{16,24},{20,28},{24,0},{28,4},{1,9},{5... | collective-permute-start | bytes 393224 | tf_op jit(solution)/shard_map/ppermute | solution.py:86
  34.0 9.8 %collective-permute-start.3 = (bf16[32,2048]{1,0:T(8,128)(2,1)S(1)}, bf16[32,2048]{1,0:T(8,128)(2,1)S(1)}, u32[]{:S(2)}, u32[]{:S(2)}) collective-permute-start(bf16[32,2048]{1,0:T(8,128)(2,1)S(1)} %get-tuple-element.24), channel_id=1, source_target_pairs={{0,1},{1,0},{2,3},{3,2},{4,5},{5,4},{6,7},{7,6},{8,9},{9,8},{10,11... | collective-permute-start | bytes 393224 | tf_op jit(solution)/shard_map/ppermute | solution.py:52
  37.1 8.2 %collective-permute-start.5 = (bf16[32,2048]{1,0:T(8,128)(2,1)S(1)}, bf16[32,2048]{1,0:T(8,128)(2,1)S(1)}, u32[]{:S(2)}, u32[]{:S(2)}) collective-permute-start(bf16[32,2048]{1,0:T(8,128)(2,1)S(1)} %get-tuple-element.25), channel_id=1, source_target_pairs={{0,3},{1,2},{2,1},{3,0},{4,7},{5,6},{6,5},{7,4},{8,11},{9,10},{10,... | collective-permute-start | bytes 393224 | tf_op jit(solution)/shard_map/ppermute | solution.py:52
  39.6 7.1 %collective-permute-start.4 = (bf16[32,2048]{1,0:T(8,128)(2,1)S(1)}, bf16[32,2048]{1,0:T(8,128)(2,1)S(1)}, u32[]{:S(2)}, u32[]{:S(2)}) collective-permute-start(bf16[32,2048]{1,0:T(8,128)(2,1)S(1)} %get-tuple-element.26), channel_id=1, source_target_pairs={{0,2},{1,3},{2,0},{3,1},{4,6},{5,7},{6,4},{7,5},{8,10},{9,11},{10,... | collective-permute-start | bytes 393224 | tf_op jit(solution)/shard_map/ppermute | solution.py:52
  41.0 18.0 %collective-permute-start.13 = (bf16[128,512]{1,0:T(8,128)(2,1)S(1)}, bf16[128,512]{1,0:T(8,128)(2,1)S(1)}, u32[]{:S(2)}, u32[]{:S(2)}) collective-permute-start(bf16[128,512]{1,0:T(8,128)(2,1)S(1)} %collective-permute-done.12), channel_id=1, source_target_pairs={{0,8},{4,12},{8,16},{12,20},{16,24},{20,28},{24,0},{28,4},{1,9},{5... | collective-permute-start | bytes 393224 | tf_op jit(solution)/shard_map/ppermute | solution.py:86
  43.8 14.2 %collective-permute-start.25 = (bf16[128,512]{1,0:T(8,128)(2,1)S(1)}, bf16[128,512]{1,0:T(8,128)(2,1)S(1)}, u32[]{:S(2)}, u32[]{:S(2)}) collective-permute-start(bf16[128,512]{1,0:T(8,128)(2,1)S(1)} %collective-permute-done.24), channel_id=1, source_target_pairs={{0,8},{4,12},{8,16},{12,20},{16,24},{20,28},{24,0},{28,4},{1,9},{5... | collective-permute-start | bytes 393224 | tf_op jit(solution)/shard_map/ppermute | solution.py:86
  43.8 10.1 %collective-permute-start.21 = (bf16[128,512]{1,0:T(8,128)(2,1)S(1)}, bf16[128,512]{1,0:T(8,128)(2,1)S(1)}, u32[]{:S(2)}, u32[]{:S(2)}) collective-permute-start(bf16[128,512]{1,0:T(8,128)(2,1)S(1)} %collective-permute-done.20), channel_id=1, source_target_pairs={{0,8},{4,12},{8,16},{12,20},{16,24},{20,28},{24,0},{28,4},{1,9},{5... | collective-permute-start | bytes 393224 | tf_op jit(solution)/shard_map/ppermute | solution.py:86
  45.2 11.5 %collective-permute-start.17 = (bf16[128,512]{1,0:T(8,128)(2,1)S(1)}, bf16[128,512]{1,0:T(8,128)(2,1)S(1)}, u32[]{:S(2)}, u32[]{:S(2)}) collective-permute-start(bf16[128,512]{1,0:T(8,128)(2,1)S(1)} %collective-permute-done.16), channel_id=1, source_target_pairs={{0,8},{4,12},{8,16},{12,20},{16,24},{20,28},{24,0},{28,4},{1,9},{5... | collective-permute-start | bytes 393224 | tf_op jit(solution)/shard_map/ppermute | solution.py:86
  53.9 12.7 %collective-permute-start.22 = (bf16[128,512]{1,0:T(8,128)(2,1)S(1)}, bf16[128,512]{1,0:T(8,128)(2,1)S(1)}, u32[]{:S(2)}, u32[]{:S(2)}) collective-permute-start(bf16[128,512]{1,0:T(8,128)(2,1)S(1)} %collective-permute-done.21), channel_id=1, source_target_pairs={{0,8},{4,12},{8,16},{12,20},{16,24},{20,28},{24,0},{28,4},{1,9},{5... | collective-permute-start | bytes 393224 | tf_op jit(solution)/shard_map/ppermute | solution.py:86
  56.7 6.8 %collective-permute-start.18 = (bf16[128,512]{1,0:T(8,128)(2,1)S(1)}, bf16[128,512]{1,0:T(8,128)(2,1)S(1)}, u32[]{:S(2)}, u32[]{:S(2)}) collective-permute-start(bf16[128,512]{1,0:T(8,128)(2,1)S(1)} %collective-permute-done.17), channel_id=1, source_target_pairs={{0,8},{4,12},{8,16},{12,20},{16,24},{20,28},{24,0},{28,4},{1,9},{5... | collective-permute-start | bytes 393224 | tf_op jit(solution)/shard_map/ppermute | solution.py:86
  58.0 9.4 %collective-permute-start.26 = (bf16[128,512]{1,0:T(8,128)(2,1)S(1)}, bf16[128,512]{1,0:T(8,128)(2,1)S(1)}, u32[]{:S(2)}, u32[]{:S(2)}) collective-permute-start(bf16[128,512]{1,0:T(8,128)(2,1)S(1)} %collective-permute-done.25), channel_id=1, source_target_pairs={{0,8},{4,12},{8,16},{12,20},{16,24},{20,28},{24,0},{28,4},{1,9},{5... | collective-permute-start | bytes 393224 | tf_op jit(solution)/shard_map/ppermute | solution.py:86
  59.0 7.3 %collective-permute-start.14 = (bf16[128,512]{1,0:T(8,128)(2,1)S(1)}, bf16[128,512]{1,0:T(8,128)(2,1)S(1)}, u32[]{:S(2)}, u32[]{:S(2)}) collective-permute-start(bf16[128,512]{1,0:T(8,128)(2,1)S(1)} %collective-permute-done.13), channel_id=1, source_target_pairs={{0,8},{4,12},{8,16},{12,20},{16,24},{20,28},{24,0},{28,4},{1,9},{5... | collective-permute-start | bytes 393224 | tf_op jit(solution)/shard_map/ppermute | solution.py:86
  63.7 5.8 %collective-permute-start.19 = (bf16[256,512]{1,0:T(8,128)(2,1)S(1)}, bf16[256,512]{1,0:T(8,128)(2,1)S(1)}, u32[]{:S(2)}, u32[]{:S(2)}) collective-permute-start(bf16[256,512]{1,0:T(8,128)(2,1)S(1)} %fusion.5), channel_id=1, source_target_pairs={{0,4},{4,0},{8,12},{12,8},{16,20},{20,16},{24,28},{28,24},{1,5},{5... | collective-permute-start | bytes 786440 | tf_op jit(solution)/shard_map/ppermute | solution.py:52
  (9 other events, 66.9 us)
